TPU v7x, 32 devices: a whole 2x2x4 slice. The times are simulated.
32 devices in a mesh: row: 8 (over y, x, core), col: 4 (over z).
Axes of the slice: x: 2, y: 2, z: 4, core: 2. Of those that a mesh axis runs over, the one named last changes fastest.
Arguments:
- pair_factors: float32 [12288, 1024], P(('row', 'col')), may hold values from -0.09375 to 0.09375
- k_prev: float32 [12288, 12288], P('row', 'col'), as said below
- energies: float32 [12288], P('row'), may hold values from 0.3 to 2
Outputs:
- casida: float32 [12288, 12288], P('row', 'col')
- vectors: float32 [12288, 8], P('row')
- images: float32 [12288, 8], P('row')
- tridiagonal: float32 [2, 8], replicated
Inputs may be any that keep to these rules, and one draw needn't show every extreme that they name: k_prev is exactly symmetric.
All inputs are finite; a program needn't handle non-finite values.
Results may differ from a plain program's by a relative error of at most 0.0003.
Values sent between devices are 32-bit elements; how exact they have to be, the bound alone decides.
No kernel may reach another device: no remote copies, remote signals or barrier semaphores. Data moves between devices by JAX's collectives and lax.ppermute only.
A program may use at most 128 MiB of HBM per device.

v0:
```python
import jax
import jax.numpy as jnp
from jax import lax
from jax.sharding import PartitionSpec as P

N = 12288
PANEL_W = 512
PC = 8


def from_root(value, axis, root):
    mine = lax.axis_index(axis) == root
    return lax.psum(jnp.where(mine, value, jnp.zeros_like(value)), axis)


def shards(pair_factors, k_prev, energies):
    rows_here, cols_here = k_prev.shape
    per_col = lax.axis_size("row") // lax.axis_size("col")
    row_index = lax.axis_index("row")
    col_index = lax.axis_index("col")
    total = jnp.zeros((rows_here, cols_here), jnp.float32)
    aux_here = pair_factors.shape[1]
    width = PANEL_W
    for start_at in range(0, aux_here, width):
        stop_at = min(start_at + width, aux_here)
        piece = pair_factors[:, start_at:stop_at]
        left_rows = lax.all_gather(piece, "col", axis=0, tiled=True)
        right_parts = []
        for offset in range(per_col):
            right_parts.append(from_root(left_rows, "row", per_col * col_index + offset))
        right_rows = jnp.concatenate(right_parts, axis=0)
        total = total + lax.dot_general(
            left_rows,
            right_rows,
            (((1,), (1,)), ((), ())),
            precision=lax.Precision.HIGHEST,
            preferred_element_type=jnp.float32,
        )
    global_rows = row_index * rows_here + jnp.arange(rows_here, dtype=jnp.int32)
    global_cols = col_index * cols_here + jnp.arange(cols_here, dtype=jnp.int32)
    on_diagonal = global_rows[:, None] == global_cols[None, :]
    casida = 4.0 * (k_prev + total) + jnp.where(on_diagonal, energies[:, None], 0.0)
    col_ids = jnp.arange(PC, dtype=jnp.int32)
    scale = jnp.sqrt(jnp.float32(N))
    diag_list = []
    sub_list = []
    spread = from_root(casida[:, :PC], "col", 0)
    panel = lax.all_gather(spread, "row", axis=0, tiled=True)
    total_rows = panel.shape[0]
    all_rows = jnp.arange(total_rows, dtype=jnp.int32)
    upper_full = jnp.zeros((total_rows, PC), jnp.float32)
    lower_full = jnp.zeros((total_rows, PC), jnp.float32)
    for column_at in range(PC):
        column = (
            panel[:, column_at]
            - jnp.dot(upper_full, lower_full[column_at], precision=lax.Precision.HIGHEST)
            - jnp.dot(lower_full, upper_full[column_at], precision=lax.Precision.HIGHEST)
        )
        diag_list.append(column[column_at])
        below = jnp.where(all_rows > column_at, column, 0.0)
        lead = column[column_at + 1]
        sigma = jnp.sum(below * below)
        root = jnp.sqrt(sigma)
        alpha = jnp.where(lead >= 0, -root, root)
        length = jnp.sqrt(jnp.maximum(2.0 * (sigma + jnp.abs(lead) * root), 1.0))
        unit = (below - alpha * (all_rows == column_at + 1).astype(jnp.float32)) / length
        unit_cols = lax.dynamic_slice_in_dim(unit, col_index * cols_here, cols_here, 0)
        partial_rows = jnp.dot(casida, unit_cols, precision=lax.Precision.HIGHEST)
        placed = lax.dynamic_update_slice_in_dim(
            jnp.zeros((total_rows,), jnp.float32), partial_rows, row_index * rows_here, 0
        )
        image = lax.psum(placed, ("row", "col"))
        image = image - jnp.dot(
            upper_full,
            jnp.dot(lower_full.T, unit, precision=lax.Precision.HIGHEST),
            precision=lax.Precision.HIGHEST,
        )
        image = image - jnp.dot(
            lower_full,
            jnp.dot(upper_full.T, unit, precision=lax.Precision.HIGHEST),
            precision=lax.Precision.HIGHEST,
        )
        image = 2.0 * image
        partner = image - jnp.sum(image * unit) * unit
        pick = (col_ids == column_at).astype(jnp.float32)[None, :]
        upper_full = upper_full + unit[:, None] * pick
        lower_full = lower_full + partner[:, None] * pick
        sub_list.append(alpha)
    upper = lax.dynamic_slice_in_dim(upper_full, row_index * rows_here, rows_here, 0)
    lower = lax.dynamic_slice_in_dim(lower_full, row_index * rows_here, rows_here, 0)
    tridiagonal = jnp.stack([jnp.stack(diag_list), jnp.stack(sub_list)])
    return (casida, scale * upper, scale * lower, tridiagonal)


def solution(mesh):
    in_specs = (P(("row", "col"), None), P("row", "col"), P("row"))
    out_specs = (P("row", "col"), P("row", None), P("row", None), P())
    return jax.shard_map(shards, mesh=mesh, in_specs=in_specs, out_specs=out_specs, check_vma=False)
```

profile of v0, /device:TPU:0, one launch (start us, length us, event | category | flops | bytes accessed | tf_op | source)
XLA Modules:
  0.0 965.7 jit_solution(18281307544850483089)
XLA Ops:
  7.2 2.6 fusion.234
  10.7 65.6 %all-gather.5.cloned.1.call-done = f32[1536,512]{1,0:T(8,128)} async-done(((f32[384,512]{1,0:T(8,128)}), f32[1536,512]{1,0:T(8,128)}) %all-gather.5.cloned.1.call-update) | async-done | bytes 3145744 | tf_op jit(solution)/shard_map/all_gather | solution.py:27
  76.3 5.6 broadcast_select_fusion.1
  81.9 58.1 %all-gather.3.cloned.1.call-done = f32[1536,512]{1,0:T(8,128)} async-done(((f32[384,512]{1,0:T(8,128)}), f32[1536,512]{1,0:T(8,128)}) %all-gather.3.cloned.1.call-update) | async-done | bytes 3145744 | tf_op jit(solution)/shard_map/all_gather | solution.py:27
  140.0 5.6 broadcast_select_fusion.3
  146.3 18.8 %copy.9 = f32[1536,3072]{0,1:T(8,128)} copy(f32[1536,3072]{1,0:T(8,128)} %param.4) | data formatting | bytes 37748736 | tf_op args[1]
  165.1 151.2 %all-reduce.3.cloned.1.call-done = (f32[1536,512]{1,0:T(8,128)}, f32[1536,512]{1,0:T(8,128)}, f32[1536,512]{1,0:T(8,128)}, f32[1536,512]{1,0:T(8,128)}) async-done(((f32[1536,512]{1,0:T(8,128)}, f32[1536,512]{1,0:T(8,128)}, f32[1536,512]{1,0:T(8,128)}, f32[1536,512]{1,0:T(8,128)}), (f32[1536,512]{1,0:T(8,128)}, f32[1536,512]{1,0:T(8,128)}, f32[1536,512]{1,0:T(8,128)}, ...) | async-done | bytes 12582928 | tf_op jit(solution)/shard_map/psum | solution.py:13
  316.4 34.6 %fusion.2 = f32[3072,1536]{1,0:T(8,128)} fusion(f32[1536,512]{1,0:T(8,128)S(1)} %copy-done.1, f32[1536,512]{1,0:T(8,128)} %get-tuple-element.12, f32[1536,512]{1,0:T(8,128)} %get-tuple-element.13), kind=kOutput, calls=%fused_computation.3 | convolution fusion | flops 28992602112 | bytes 28311552 | tf_op jit(solution)/shard_map/dot_general | solution.py:32
  351.0 38.9 %fusion.1 = f32[1536,3072]{0,1:T(8,128)S(1)} fusion(f32[1536,3072]{0,1:T(8,128)} %copy.9, f32[3072,1536]{1,0:T(8,128)} %fusion.2, f32[1536,512]{1,0:T(8,128)} %all-gather.5.cloned.1.call-done, f32[1536]{0:T(1024)S(1)} %copy-done.2, s32[1536]{0:T(1024)S(1)} %iota_add_fusion.1, s32[3072]{0:T(1024)S(1)} %iota_add_fusion, f32[1536,512]{1,0:T(8,128)} %get-tuple-element.14, ...), kind=kOutput, calls=%fused_computation.2 | convolution fusion | flops 29020913664 | bytes 66084864 | tf_op jit(solution)/shard_map/dot_general | solution.py:32
  389.9 6.5 copy-done
  396.4 19.5 %psum.95 = f32[1536,8]{0,1:T(8,128)S(1)} all-reduce(f32[1536,8]{0,1:T(8,128)S(1)} %slice_select_fusion), channel_id=1, replica_groups=mesh['row'=8,'col'=4] {'col'}, use_global_device_ids=true, to_apply=%region_4.5 | all-reduce | flops 12288 | bytes 98304 | tf_op jit(solution)/shard_map/psum | solution.py:13
  415.9 9.5 all_gather.11
  430.3 12.9 %convolution_reduce_fusion.7 = f32[1536]{0:T(1024)S(1)} fusion(f32[1536,3072]{0,1:T(8,128)} %copy-done, f32[3072,1]{0,1:T(1,128)S(1)} %bitcast.304), kind=kOutput, calls=%fused_computation.21 | convolution fusion | flops 56623104 | bytes 18892800 | tf_op jit(solution)/shard_map/dot_general | solution.py:68
  443.5 38.1 %psum.96 = f32[12288]{0:T(1024)S(1)} all-reduce(f32[12288]{0:T(1024)S(1)} %dynamic_update_slice.24), channel_id=1, replica_groups=mesh['row'=8,'col'=4] {'row','col'}, use_global_device_ids=true, to_apply=%region_6.7 | all-reduce | flops 12288 | bytes 98304 | tf_op jit(solution)/shard_map/psum | solution.py:72
  481.6 1.6 fusion.12
  490.5 1.0 convolution_bitcast_fusion.13
  491.5 1.0 convolution_bitcast_fusion.12
  493.1 12.9 %convolution_reduce_fusion.6 = f32[1536]{0:T(1024)S(1)} fusion(f32[1536,3072]{0,1:T(8,128)} %copy-done, f32[3072,1]{0,1:T(1,128)S(1)} %bitcast.298), kind=kOutput, calls=%fused_computation.20 | convolution fusion | flops 56623104 | bytes 18892800 | tf_op jit(solution)/shard_map/dot_general | solution.py:68
  506.3 41.5 %psum.97 = f32[12288]{0:T(1024)S(1)} all-reduce(f32[12288]{0:T(1024)S(1)} %dynamic_update_slice.25), channel_id=1, replica_groups=mesh['row'=8,'col'=4] {'row','col'}, use_global_device_ids=true, to_apply=%region_9.10 | all-reduce | flops 12288 | bytes 98304 | tf_op jit(solution)/shard_map/psum | solution.py:72
  555.2 1.0 convolution_bitcast_fusion.11
  556.2 1.0 convolution_bitcast_fusion.10
  557.9 12.9 %convolution_reduce_fusion.5 = f32[1536]{0:T(1024)S(1)} fusion(f32[1536,3072]{0,1:T(8,128)} %copy-done, f32[3072,1]{0,1:T(1,128)S(1)} %bitcast.299), kind=kOutput, calls=%fused_computation.19 | convolution fusion | flops 56623104 | bytes 18892800 | tf_op jit(solution)/shard_map/dot_general | solution.py:68
  571.1 40.2 %psum.98 = f32[12288]{0:T(1024)S(1)} all-reduce(f32[12288]{0:T(1024)S(1)} %dynamic_update_slice.26), channel_id=1, replica_groups=mesh['row'=8,'col'=4] {'row','col'}, use_global_device_ids=true, to_apply=%region_12.13 | all-reduce | flops 12288 | bytes 98304 | tf_op jit(solution)/shard_map/psum | solution.py:72
  618.7 1.0 convolution_bitcast_fusion.9
  619.8 1.0 convolution_bitcast_fusion.8
  621.4 12.9 %convolution_reduce_fusion.4 = f32[1536]{0:T(1024)S(1)} fusion(f32[1536,3072]{0,1:T(8,128)} %copy-done, f32[3072,1]{0,1:T(1,128)S(1)} %bitcast.300), kind=kOutput, calls=%fused_computation.18 | convolution fusion | flops 56623104 | bytes 18892800 | tf_op jit(solution)/shard_map/dot_general | solution.py:68
  634.6 41.1 %psum.99 = f32[12288]{0:T(1024)S(1)} all-reduce(f32[12288]{0:T(1024)S(1)} %dynamic_update_slice.27), channel_id=1, replica_groups=mesh['row'=8,'col'=4] {'row','col'}, use_global_device_ids=true, to_apply=%region_15.16 | all-reduce | flops 12288 | bytes 98304 | tf_op jit(solution)/shard_map/psum | solution.py:72
  683.5 1.0 convolution_bitcast_fusion.7
  684.5 1.0 convolution_bitcast_fusion.6
  686.2 12.9 %convolution_reduce_fusion.3 = f32[1536]{0:T(1024)S(1)} fusion(f32[1536,3072]{0,1:T(8,128)} %copy-done, f32[3072,1]{0,1:T(1,128)S(1)} %bitcast.301), kind=kOutput, calls=%fused_computation.17 | convolution fusion | flops 56623104 | bytes 18892800 | tf_op jit(solution)/shard_map/dot_general | solution.py:68
  699.4 40.0 %psum.100 = f32[12288]{0:T(1024)S(1)} all-reduce(f32[12288]{0:T(1024)S(1)} %dynamic_update_slice.28), channel_id=1, replica_groups=mesh['row'=8,'col'=4] {'row','col'}, use_global_device_ids=true, to_apply=%region_18.19 | all-reduce | flops 12288 | bytes 98304 | tf_op jit(solution)/shard_map/psum | solution.py:72
  747.1 1.0 convolution_bitcast_fusion.5
  748.1 1.0 convolution_bitcast_fusion.4
  749.8 12.9 %convolution_reduce_fusion.2 = f32[1536]{0:T(1024)S(1)} fusion(f32[1536,3072]{0,1:T(8,128)} %copy-done, f32[3072,1]{0,1:T(1,128)S(1)} %bitcast.302), kind=kOutput, calls=%fused_computation.16 | convolution fusion | flops 56623104 | bytes 18892800 | tf_op jit(solution)/shard_map/dot_general | solution.py:68
  763.0 41.2 %psum.101 = f32[12288]{0:T(1024)S(1)} all-reduce(f32[12288]{0:T(1024)S(1)} %dynamic_update_slice.29), channel_id=1, replica_groups=mesh['row'=8,'col'=4] {'row','col'}, use_global_device_ids=true, to_apply=%region_21.22 | all-reduce | flops 12288 | bytes 98304 | tf_op jit(solution)/shard_map/psum | solution.py:72
  811.8 1.0 convolution_bitcast_fusion.3
  812.8 1.0 convolution_bitcast_fusion.2
  814.3 12.9 %convolution_reduce_fusion.1 = f32[1536]{0:T(1024)S(1)} fusion(f32[1536,3072]{0,1:T(8,128)} %copy-done, f32[3072,1]{0,1:T(1,128)S(1)} %bitcast.303), kind=kOutput, calls=%fused_computation.15 | convolution fusion | flops 56623104 | bytes 18892800 | tf_op jit(solution)/shard_map/dot_general | solution.py:68
  827.5 40.1 %psum.102 = f32[12288]{0:T(1024)S(1)} all-reduce(f32[12288]{0:T(1024)S(1)} %dynamic_update_slice.30), channel_id=1, replica_groups=mesh['row'=8,'col'=4] {'row','col'}, use_global_device_ids=true, to_apply=%region_24.25 | all-reduce | flops 12288 | bytes 98304 | tf_op jit(solution)/shard_map/psum | solution.py:72
  874.7 1.1 convolution_bitcast_fusion.1
  875.8 1.1 convolution_bitcast_fusion
  876.9 18.6 %copy.10 = f32[1536,3072]{1,0:T(8,128)} copy(f32[1536,3072]{0,1:T(8,128)} %copy-done) | data formatting | bytes 37748736
  896.0 12.9 %convolution_reduce_fusion = f32[1536]{0:T(1024)S(1)} fusion(f32[1536,3072]{0,1:T(8,128)} %copy-done, f32[3072,1]{0,1:T(1,128)S(1)} %bitcast.297), kind=kOutput, calls=%fused_computation.14 | convolution fusion | flops 56623104 | bytes 18892800 | tf_op jit(solution)/shard_map/dot_general | solution.py:68
  909.2 41.0 %psum.103 = f32[12288]{0:T(1024)S(1)} all-reduce(f32[12288]{0:T(1024)S(1)} %dynamic_update_slice.31), channel_id=1, replica_groups=mesh['row'=8,'col'=4] {'row','col'}, use_global_device_ids=true, to_apply=%region_27.28 | all-reduce | flops 12288 | bytes 98304 | tf_op jit(solution)/shard_map/psum | solution.py:72
  950.7 0.7 multiply_reduce_fusion
  951.4 0.7 multiply_subtract_fusion
  952.2 5.1 stack.39
  957.9 0.7 fusion.195
  (140 shorter events, 44.9 us)
Async XLA Ops:
  7.2 69.2 %all-gather.5.cloned.1.call-start = ((), (), s32[]{:S(2)}) async-start(), calls=%async_computation.1 | async-start | bytes 3932160 | tf_op jit(solution)/shard_map/all_gather | solution.py:27
  9.9 130.1 %all-gather.3.cloned.1.call-start = ((), (), s32[]{:S(2)}) async-start(), calls=%async_computation | async-start | bytes 3932160 | tf_op jit(solution)/shard_map/all_gather | solution.py:27
  10.6 305.7 %all-reduce.3.cloned.1.call-start = ((), (), s32[]{:S(2)}) async-start(), calls=%async_computation.2 | async-start | bytes 25165824 | tf_op jit(solution)/shard_map/psum | solution.py:13
  146.3 170.1 %copy-start.1 = (f32[1536,512]{1,0:T(8,128)S(1)}, f32[1536,512]{1,0:T(8,128)}, u32[]{:S(2)}) copy-start(f32[1536,512]{1,0:T(8,128)} %all-gather.3.cloned.1.call-done) | copy-start | bytes 9437188
  165.0 185.9 %copy-start.2 = (f32[1536]{0:T(1024)S(1)}, f32[1536]{0:T(1024)}, u32[]{:S(2)}) copy-start(f32[1536]{0:T(1024)} %param.5) | copy-start | bytes 18436
  389.9 6.5 copy-start
Sparse Core Ops, SparseCore 0:
  10.1 66.1 all-gather.4
  77.9 62.0 all-gather.2
  145.7 170.6 all-reduce.2
where the time goes:
time: 974 us; the launch traced here: 966 us
  blocking collectives  352 us (36%)
  waiting for transfers between devices  276 us (28%)
  matrix products  208 us (21%)
  local copies, waits for them, and re-layouts  63.6 us (7%)
  between operations  36 us (4%)
  other arithmetic  30 us (3%)
    psum x8, blocking collectives, shards(): image = lax.psum(placed, ('row', 'col'))  323 us
    psum x1, waiting for transfers between devices, from_root(): return lax.psum(jnp.where(mine, value, jnp.zeros_like(value)), axis)  151 us
    all_gather x2, waiting for transfers between devices, shards(): left_rows = lax.all_gather(piece, 'col', axis=0, tiled=True)  124 us
    dot_general x8, matrix products, shards(): partial_rows = jnp.dot(casida, unit_cols, precision=lax.Precision.HIGHEST)  103 us
    dot_general x2, matrix products, shards(): lax.dot_general(left_rows, right_rows, (((1,), (1,)), ((), ())), precisio...  73.6 us
    unnamed x8, local copies, waits for them, and re-layouts  43.9 us
  transfers between devices with their start and end apart: 3, of which 3 were waited for; matrix products, arithmetic and copies ran while one was open for 3% of the time, Pallas kernels for 0%

commit v1 on v0

v1 whole, which is shorter than its diff:
```python
import functools
import math

import jax
import jax.numpy as jnp
from jax import lax
from jax.experimental import pallas as pl
from jax.experimental.pallas import tpu as pltpu
from jax.sharding import PartitionSpec as P

PC = 8
CHUNKS = 4
LANES = 128
AXES = ("row", "col")


def walk(steps, backwards):
    order = [i ^ (i >> 1) for i in range(steps)]
    return order[:1] + order[1:][::-1] if backwards else order


def forward(moving, rows, cols, step):
    group = rows // cols
    paths = [walk(cols, member % 2 == 1) for member in range(group)]
    pairs = []
    for col in range(cols):
        for member in range(group):
            source = (col ^ paths[member][step - 1]) * group + member
            target = (col ^ paths[member][step]) * group + member
            pairs.append((source * cols + col, target * cols + col))
    return lax.ppermute(moving, AXES, pairs)


def spread_rows(mine, moved, rows, cols):
    group = rows // cols
    row_index = lax.axis_index("row")
    col_index = lax.axis_index("col")
    total = jnp.where(row_index // group == col_index, mine, jnp.zeros_like(mine))
    for part in moved:
        total = total + part
    blocks = [total]
    for shift in range(1, group):
        pairs = [
            (row, (row // group) * group + (row + shift) % group) for row in range(rows)
        ]
        blocks.append(lax.ppermute(total, "row", pairs))
    member_here = row_index % group
    ordered = []
    for member in range(group):
        block = blocks[0]
        for shift in range(1, group):
            block = jnp.where((member + shift) % group == member_here, blocks[shift], block)
        ordered.append(block)
    return jnp.concatenate(ordered, axis=0)


def total_of(value):
    return jnp.sum(value, keepdims=True).reshape(1, 1)


def householder_kernel(
    column_at, group, col_ref, panel_ref, parts_ref, upper_in, lower_in, tri_in, casida_ref,
    image_ref, upper_ref, lower_ref, tri_ref, unit_ref,
):
    rows, width = panel_ref.shape[1:]

    @pl.when(pl.program_id(0) == 0)
    def _():
        index = lax.broadcasted_iota(jnp.int32, (rows, width), 0) * width
        index = index + lax.broadcasted_iota(jnp.int32, (rows, width), 1)
        last = column_at - 1
        uppers = [upper_in[i] for i in range(column_at)]
        lowers = [lower_in[i] for i in range(max(last, 0))]
        for i in range(PC):
            upper_ref[i] = upper_in[i]
            lower_ref[i] = lower_in[i]
        if column_at > 0:
            unit = uppers[last]
            image = jnp.sum(parts_ref[...], axis=0)
            fixed = image
            for i in range(last):
                fixed = fixed - uppers[i] * total_of(lowers[i] * unit) - lowers[i] * total_of(uppers[i] * unit)
            fixed = 2.0 * fixed
            partner = fixed - total_of(fixed * unit) * unit
            lower_ref[last] = partner
            lowers.append(partner)
        if column_at < PC:
            column = panel_ref[column_at]
            here = index == column_at
            for i in range(column_at):
                at_lower = total_of(jnp.where(here, lowers[i], 0.0))
                at_upper = total_of(jnp.where(here, uppers[i], 0.0))
                column = column - uppers[i] * at_lower - lowers[i] * at_upper
            diag = total_of(jnp.where(here, column, 0.0))
            below = jnp.where(index > column_at, column, 0.0)
            head = index == column_at + 1
            lead = total_of(jnp.where(head, column, 0.0))
            sigma = total_of(below * below)
            root = jnp.sqrt(sigma)
            alpha = jnp.where(lead >= 0, -root, root)
            length = jnp.sqrt(jnp.maximum(2.0 * (sigma + jnp.abs(lead) * root), 1.0))
            unit = (below - jnp.where(head, alpha, 0.0)) / length
            upper_ref[column_at] = unit
            unit_ref[...] = unit
            lane = lax.broadcasted_iota(jnp.int32, tri_in.shape, 1)
            line = lax.broadcasted_iota(jnp.int32, tri_in.shape, 0)
            tri = tri_in[...]
            tri = jnp.where((lane == column_at) & (line == 0), diag, tri)
            tri_ref[...] = jnp.where((lane == column_at) & (line == 1), alpha, tri)
        else:
            tri_ref[...] = tri_in[...]

    if column_at < PC:
        acc = jnp.zeros((casida_ref.shape[0], LANES), jnp.float32)
        first = col_ref[0] * group
        for member in range(group):
            unit = unit_ref[pl.ds(first + member, 1), :]
            for start in range(0, width, LANES):
                at = member * width + start
                acc = acc + casida_ref[:, at : at + LANES] * unit[:, start : start + LANES]
        ones = jnp.ones((8, LANES), jnp.bfloat16)
        sums = jnp.zeros((8, casida_ref.shape[0]), jnp.float32)
        for _ in range(3):
            term = acc.astype(jnp.bfloat16)
            acc = acc - term.astype(jnp.float32)
            sums = sums + lax.dot_general(
                ones, term, (((1,), (1,)), ((), ())), preferred_element_type=jnp.float32
            )
        image_ref[...] = sums[0:1]


def householder(column_at, group, block, col, panel, parts, upper, lower, tri, casida):
    rows_here = casida.shape[0]
    last = column_at == PC
    whole = lambda x: pl.BlockSpec(x.shape, lambda i, c, n=x.ndim: (0,) * n)
    grid = (1,) if last else (rows_here // block,)
    return pl.pallas_call(
        functools.partial(householder_kernel, column_at, group),
        grid_spec=pltpu.PrefetchScalarGridSpec(
            num_scalar_prefetch=1,
            grid=grid,
            in_specs=[
                whole(panel), whole(parts), whole(upper), whole(lower), whole(tri),
                pl.BlockSpec((block, casida.shape[1]), lambda i, c: (i, 0)),
            ],
            out_specs=[
                pl.BlockSpec((1, block), lambda i, c: (0, i)),
                whole(upper), whole(lower), whole(tri),
            ],
            scratch_shapes=[pltpu.VMEM(panel.shape[1:], jnp.float32)],
        ),
        out_shape=[
            jax.ShapeDtypeStruct((1, rows_here), jnp.float32),
            jax.ShapeDtypeStruct(upper.shape, jnp.float32),
            jax.ShapeDtypeStruct(lower.shape, jnp.float32),
            jax.ShapeDtypeStruct(tri.shape, jnp.float32),
        ],
        name=f"reflect{column_at}",
    )(col, panel, parts, upper, lower, tri, casida)


def to_all(value, count):
    return lax.all_to_all(jnp.broadcast_to(value, (count,) + value.shape), AXES, 0, 0)


def shards(pair_factors, k_prev, energies):
    rows = lax.axis_size("row")
    cols = lax.axis_size("col")
    group = rows // cols
    rows_here, cols_here = k_prev.shape
    row_index = lax.axis_index("row")
    col_index = lax.axis_index("col")
    aux_here = pair_factors.shape[1]
    width = aux_here // CHUNKS
    pieces = [pair_factors[:, at : at + width] for at in range(0, aux_here, width)]
    global_rows = row_index * rows_here + jnp.arange(rows_here, dtype=jnp.int32)
    global_cols = col_index * cols_here + jnp.arange(cols_here, dtype=jnp.int32)
    on_diagonal = global_rows[:, None] == global_cols[None, :]
    casida = 4.0 * k_prev + jnp.where(on_diagonal, energies[:, None], 0.0)
    lefts = []
    moves = []
    for at, piece in enumerate(pieces):
        if at >= 2:
            first = [moves[i][at - 2 - i] for i in range(at - 1) if at - 2 - i < len(moves[i])]
            piece, first = lax.optimization_barrier((piece, first))
            for i in range(at - 1):
                if at - 2 - i < len(moves[i]):
                    moves[i][at - 2 - i] = first.pop(0)
        lefts.append(lax.all_gather(piece, "col", axis=0, tiled=True))
        moves.append([])
        for i in range(at + 1):
            if len(moves[i]) < cols - 1:
                moves[i].append(forward(moves[i][-1] if moves[i] else lefts[i], rows, cols, len(moves[i]) + 1))
    for left, moved in zip(lefts, moves):
        while len(moved) < cols - 1:
            moved.append(forward(moved[-1], rows, cols, len(moved) + 1))
        right = spread_rows(left, moved, rows, cols)
        casida = casida + lax.dot_general(
            4.0 * left, right, (((1,), (1,)), ((), ())),
            precision=lax.Precision.HIGH, preferred_element_type=jnp.float32,
        )

    lead = casida[:, :PC].T
    spread = jnp.where(col_index == 0, lead, 0.0)
    for target in range(1, cols):
        spread = spread + lax.ppermute(lead, "col", [(0, target)])
    panel = jnp.swapaxes(lax.all_gather(spread, "row", axis=0, tiled=False), 0, 1)
    upper = jnp.zeros((PC, rows, rows_here), jnp.float32)
    lower = jnp.zeros((PC, rows, rows_here), jnp.float32)
    tri = jnp.zeros((8, LANES), jnp.float32)
    parts = jnp.zeros((cols, rows, rows_here), jnp.float32)
    col = col_index.reshape(1).astype(jnp.int32)
    block = LANES * math.gcd(rows_here // LANES, 2)
    for column_at in range(PC + 1):
        image, upper, lower, tri = householder(
            column_at, group, block, col, panel, parts, upper, lower, tri, casida
        )
        if column_at < PC:
            parts = to_all(image.reshape(rows_here), rows * cols)
            parts = jnp.swapaxes(parts.reshape(rows, cols, rows_here), 0, 1)
    scale = jnp.sqrt(jnp.float32(rows * rows_here))
    pick = lambda x: scale * lax.dynamic_index_in_dim(x, row_index, 1, keepdims=False).T
    return (casida, pick(upper), pick(lower), tri[:2, :PC])


def solution(mesh):
    in_specs = (P(("row", "col"), None), P("row", "col"), P("row"))
    out_specs = (P("row", "col"), P("row", None), P("row", None), P())
    return jax.shard_map(shards, mesh=mesh, in_specs=in_specs, out_specs=out_specs, check_vma=False)
```

time: 974 us -> 512 us (0.53)
  blocking collectives: 352 us -> 91 us
  matrix products: 208 us -> 66.8 us
  waiting for transfers between devices: 276 us -> 154 us
  Pallas kernels: 0 us -> 80.7 us
  starting transfers between devices: 0.12 us -> 58.5 us
  local copies, waits for them, and re-layouts: 63.6 us -> 19.2 us
  between operations: 36 us -> 14.2 us
    psum x9 -> x0, blocking collectives: 343 us -> none  [the longest x8 323 us: shards(): image = lax.psum(placed, ('row', 'col'))]
    psum x1 -> x0, waiting for transfers between devices: 151 us -> none  [from_root(): return lax.psum(jnp.where(mine, value, jnp.zeros_like(value)), axis)]
    dot_general x53 -> x4, matrix products: 208 us -> 66.8 us  [shards(): lax.dot_general(4.0 * left, right, (((1,), (1,)), ((), ())), precision=la...]
    all_to_all x0 -> x7, blocking collectives: none -> 82.8 us  [to_all(): lax.all_to_all(jnp.broadcast_to(value, (count,) + value.shape), AXES, 0, 0)]
    pallas_call x0 -> x9, Pallas kernels: none -> 80.7 us  [householder(): pl.pallas_call(functools.partial(householder_kernel, column_at, group), g...]
    ppermute x0 -> x19, starting transfers between devices: none -> 55.8 us  [the longest x12 27.7 us: forward(): return lax.ppermute(moving, AXES, pairs)]
    ppermute x0 -> x19, waiting for transfers between devices: none -> 44.3 us  [the longest x12 44.3 us: forward(): return lax.ppermute(moving, AXES, pairs)]
    unnamed x8 -> x16, local copies, waits for them, and re-layouts: 43.9 us -> 1.97 us
  transfers between devices with their start and end apart: 3 -> 24, of which waited for: 3 -> 8; matrix products, arithmetic and copies ran while one was open for 3% -> 9% of each run, Pallas kernels for 0% -> 0%
where the time goes in v1:
time: 512 us; the launch traced here: 511 us
  waiting for transfers between devices  154 us (30%)
  blocking collectives  91 us (18%)
  Pallas kernels  80.7 us (16%)
  matrix products  66.8 us (13%)
  starting transfers between devices  58.5 us (11%)
  other arithmetic  25.6 us (5%)
  local copies, waits for them, and re-layouts  19.2 us (4%)
  between operations  14.2 us (3%)
    all_gather x4, waiting for transfers between devices, shards(): lefts.append(lax.all_gather(piece, 'col', axis=0, tiled=True))  100 us
    all_to_all x7, blocking collectives, to_all(): lax.all_to_all(jnp.broadcast_to(value, (count,) + value.shape), AXES, 0, 0)  82.8 us
    pallas_call x9, Pallas kernels, householder(): pl.pallas_call(functools.partial(householder_kernel, column_at, group), g...  80.7 us
    dot_general x4, matrix products, shards(): lax.dot_general(4.0 * left, right, (((1,), (1,)), ((), ())), precision=la...  66.8 us
    ppermute x12, waiting for transfers between devices, forward(): return lax.ppermute(moving, AXES, pairs)  44.3 us
    ppermute x12, starting transfers between devices, forward(): return lax.ppermute(moving, AXES, pairs)  27.7 us
    ppermute x3, starting transfers between devices, shards(): spread = spread + lax.ppermute(lead, 'col', [(0, target)])  27 us
  transfers between devices with their start and end apart: 24, of which 8 were waited for; matrix products, arithmetic and copies ran while one was open for 9% of the time, Pallas kernels for 0%

profile of v1, /device:TPU:0, one launch (start us, length us, event | category | flops | bytes accessed | tf_op | source)
XLA Modules:
  0.0 510.5 jit_solution(6589518348542228315)
XLA Ops:
  7.2 2.6 fusion.34
  10.6 39.3 %all-gather.6.cloned.1.call-done = f32[1536,256]{1,0:T(8,128)} async-done(((f32[384,256]{1,0:T(8,128)}), f32[1536,256]{1,0:T(8,128)}) %all-gather.6.cloned.1.call-update) | async-done | bytes 1572880 | tf_op jit(solution)/shard_map/all_gather | solution.py:189
  49.9 3.5 collective-permute-start
  53.4 18.1 %collective-permute-done = f32[1536,256]{1,0:T(8,128)S(1)} collective-permute-done((f32[1536,256]{1,0:T(8,128)}, f32[1536,256]{1,0:T(8,128)S(1)}, u32[]{:S(2)}, u32[]{:S(2)}) %collective-permute-start) | collective-permute-done | bytes 1572896 | tf_op jit(solution)/shard_map/ppermute | solution.py:31
  71.6 15.8 %all-gather.8.cloned.1.call-done = f32[1536,256]{1,0:T(8,128)} async-done(((f32[384,256]{1,0:T(8,128)}), f32[1536,256]{1,0:T(8,128)}) %all-gather.8.cloned.1.call-update) | async-done | bytes 1572880 | tf_op jit(solution)/shard_map/all_gather | solution.py:189
  87.4 3.5 collective-permute-start.2
  90.9 1.8 collective-permute-start.1
  92.7 16.3 %collective-permute-done.2 = f32[1536,256]{1,0:T(8,128)S(1)} collective-permute-done((f32[1536,256]{1,0:T(8,128)}, f32[1536,256]{1,0:T(8,128)S(1)}, u32[]{:S(2)}, u32[]{:S(2)}) %collective-permute-start.2) | collective-permute-done | bytes 1572896 | tf_op jit(solution)/shard_map/ppermute | solution.py:31
  109.0 1.8 collective-permute-start.5
  110.8 14.1 %all-gather.10.cloned.1.call-done = f32[1536,256]{1,0:T(8,128)} async-done(((f32[384,256]{1,0:T(8,128)}), f32[1536,256]{1,0:T(8,128)}) %all-gather.10.cloned.1.call-update) | async-done | bytes 1572880 | tf_op jit(solution)/shard_map/all_gather | solution.py:189
  124.9 4.6 collective-permute-start.8
  129.5 1.8 collective-permute-start.6
  131.3 30.9 %all-gather.12.cloned.1.call-done = f32[1536,256]{1,0:T(8,128)} async-done(((f32[384,256]{1,0:T(8,128)}), f32[1536,256]{1,0:T(8,128)}) %all-gather.12.cloned.1.call-update) | async-done | bytes 1572880 | tf_op jit(solution)/shard_map/all_gather | solution.py:189
  162.2 4.5 collective-permute-start.12
  166.8 1.9 collective-permute-start.9
  168.6 1.9 collective-permute-start.3
  170.5 3.4 add_add_fusion.3
  174.0 9.8 %collective-permute-done.12 = f32[1536,256]{1,0:T(8,128)} collective-permute-done((f32[1536,256]{1,0:T(8,128)}, f32[1536,256]{1,0:T(8,128)}, u32[]{:S(2)}, u32[]{:S(2)}) %collective-permute-start.12) | collective-permute-done | bytes 1572896 | tf_op jit(solution)/shard_map/ppermute | solution.py:31
  185.4 2.8 add_add_fusion.4
  188.3 1.7 broadcast_select_fusion.6
  191.0 11.0 %fusion.4 = f32[1536,3072]{1,0:T(8,128)} fusion(f32[1536,256]{1,0:T(8,128)S(1)} %get-tuple-element.89, f32[1536,256]{1,0:T(8,128)S(1)} %get-tuple-element.88, f32[1536,256]{1,0:T(8,128)S(1)} %copy-done.3), kind=kOutput, calls=%fused_computation.5 | convolution fusion | flops 7248936960 | bytes 23592960 | tf_op jit(solution)/shard_map/dot_general | solution.py:198
  202.0 2.3 add_add_fusion.2
  205.7 1.8 add_add_fusion.1
  208.0 11.0 %fusion = f32[1536,3072]{1,0:T(8,128)} fusion(f32[1536,256]{1,0:T(8,128)S(1)} %get-tuple-element.87, f32[1536,256]{1,0:T(8,128)S(1)} %get-tuple-element.86, f32[1536,256]{1,0:T(8,128)S(1)} %copy-done.1), kind=kOutput, calls=%fused_computation.1 | convolution fusion | flops 7248936960 | bytes 23592960 | tf_op jit(solution)/shard_map/dot_general | solution.py:198
  219.1 11.0 %fusion.8 = f32[1536,3072]{1,0:T(8,128)} fusion(f32[1536,256]{1,0:T(8,128)S(1)} %get-tuple-element.91, f32[1536,256]{1,0:T(8,128)S(1)} %get-tuple-element.90, f32[1536,256]{1,0:T(8,128)S(1)} %copy-done.2), kind=kOutput, calls=%fused_computation.9 | convolution fusion | flops 7248936960 | bytes 23592960 | tf_op jit(solution)/shard_map/dot_general | solution.py:198
  230.2 1.3 broadcast_select_fusion.4
  231.5 33.8 %add_add_fusion.casida_ref = f32[1536,3072]{1,0:T(8,128)} fusion(f32[1536,3072]{1,0:T(8,128)} %fusion.8, f32[1536,3072]{1,0:T(8,128)} %fusion.4, f32[1536,3072]{1,0:T(8,128)} %fusion, f32[1536,3072]{1,0:T(8,128)} %param.4, f32[1536]{0:T(1024)S(1)} %copy-done.6, s32[3072]{0:T(1024)S(1)} %iota_add_fusion, s32[1536]{0:T(1024)S(1)} %iota_add_fusion.1, ...), kind=kOutput, calls=%fused_computation | convolution fusion | flops 7286685696 | bytes 99115008 | tf_op jit(solution)/shard_map/dot_general | solution.py:198
  266.7 24.5 %collective-permute-start.17 = (f32[8,1536]{1,0:T(8,128)S(1)}, f32[8,1536]{1,0:T(8,128)S(1)}, u32[]{:S(2)}, u32[]{:S(2)}) collective-permute-start(f32[8,1536]{1,0:T(8,128)S(1)} %copy.34), channel_id=1, source_target_pairs={{0,2},{4,6},{8,10},{12,14},{16,18},{20,22},{24,26},{28,30}} | collective-permute-start | bytes 147464 | tf_op jit(solution)/shard_map/ppermute | solution.py:206
  291.2 1.3 collective-permute-start.16
  296.1 8.2 %all-gather = f32[64,1536]{1,0:T(8,128)S(1)} all-gather(f32[8,1536]{1,0:T(8,128)S(1)} %copy.40), channel_id=2, replica_groups=mesh['row'=8,'col'=4] {'row'}, dimensions={0}, use_global_device_ids=true | all-gather | bytes 442368 | tf_op jit(solution)/shard_map/all_gather | solution.py:207
  307.4 10.0 %reflect0.1 = (f32[1,1536]{1,0:T(1,128)}, f32[8,8,1536]{2,1,0:T(8,128)}, f32[8,8,1536]{2,1,0:T(8,128)}, f32[8,128]{1,0:T(8,128)}) custom-call(s32[1]{0:T(128)} %bitcast.col_ref, f32[8,8,1536]{2,1,0:T(8,128)} %bitcast.43, f32[4,8,1536]{2,1,0:T(8,128)} %broadcast_in_dim.52.parts_ref, f32[8,8,1536]{2,1,0:T(8,128)} %broadcast_5_upper_in_lower_in.2.upper_in.lower_in, ...), custom_call_target="tpu_custom_call" | custom-call | tf_op jit(solution)/shard_map/reflect0/pallas_call | solution.py:137
  318.2 14.9 %all_to_all.48 = f32[32,1,1536]{2,1,0:T(1,128)S(1)} all-to-all(f32[32,1,1536]{2,1,0:T(1,128)S(1)} %broadcast_in_dim.54), channel_id=1, replica_groups=mesh['row'=8,'col'=4] {'row','col'}, dimensions={0} | all-to-all | bytes 393216 | tf_op jit(solution)/shard_map/all_to_all | solution.py:163
  334.5 9.4 %reflect1.1 = (f32[1,1536]{1,0:T(1,128)}, f32[8,8,1536]{2,1,0:T(8,128)}, f32[8,8,1536]{2,1,0:T(8,128)}, f32[8,128]{1,0:T(8,128)}) custom-call(s32[1]{0:T(128)} %bitcast.col_ref, f32[8,8,1536]{2,1,0:T(8,128)} %bitcast.44, f32[4,8,1536]{2,1,0:T(8,128)} %bitcast.54, f32[8,8,1536]{2,1,0:T(8,128)} %get-tuple-element.50.upper_in, ...), custom_call_target="tpu_custom_call" | custom-call | tf_op jit(solution)/shard_map/reflect1/pallas_call | solution.py:137
  344.7 11.3 %all_to_all.49 = f32[32,1,1536]{2,1,0:T(1,128)S(1)} all-to-all(f32[32,1,1536]{2,1,0:T(1,128)S(1)} %broadcast_in_dim.55), channel_id=1, replica_groups=mesh['row'=8,'col'=4] {'row','col'}, dimensions={0} | all-to-all | bytes 393216 | tf_op jit(solution)/shard_map/all_to_all | solution.py:163
  357.3 9.6 %reflect2.1 = (f32[1,1536]{1,0:T(1,128)}, f32[8,8,1536]{2,1,0:T(8,128)}, f32[8,8,1536]{2,1,0:T(8,128)}, f32[8,128]{1,0:T(8,128)}) custom-call(s32[1]{0:T(128)} %bitcast.col_ref, f32[8,8,1536]{2,1,0:T(8,128)} %bitcast.45, f32[4,8,1536]{2,1,0:T(8,128)} %bitcast.55, f32[8,8,1536]{2,1,0:T(8,128)} %get-tuple-element.54.upper_in, ...), custom_call_target="tpu_custom_call" | custom-call | tf_op jit(solution)/shard_map/reflect2/pallas_call | solution.py:137
  367.7 11.3 %all_to_all.50 = f32[32,1,1536]{2,1,0:T(1,128)S(1)} all-to-all(f32[32,1,1536]{2,1,0:T(1,128)S(1)} %broadcast_in_dim.56), channel_id=1, replica_groups=mesh['row'=8,'col'=4] {'row','col'}, dimensions={0} | all-to-all | bytes 393216 | tf_op jit(solution)/shard_map/all_to_all | solution.py:163
  380.3 9.6 %reflect3.1 = (f32[1,1536]{1,0:T(1,128)}, f32[8,8,1536]{2,1,0:T(8,128)}, f32[8,8,1536]{2,1,0:T(8,128)}, f32[8,128]{1,0:T(8,128)}) custom-call(s32[1]{0:T(128)} %bitcast.col_ref, f32[8,8,1536]{2,1,0:T(8,128)} %bitcast.46, f32[4,8,1536]{2,1,0:T(8,128)} %bitcast.56, f32[8,8,1536]{2,1,0:T(8,128)} %get-tuple-element.58.upper_in, ...), custom_call_target="tpu_custom_call" | custom-call | tf_op jit(solution)/shard_map/reflect3/pallas_call | solution.py:137
  390.8 11.3 %all_to_all.51 = f32[32,1,1536]{2,1,0:T(1,128)S(1)} all-to-all(f32[32,1,1536]{2,1,0:T(1,128)S(1)} %broadcast_in_dim.57), channel_id=1, replica_groups=mesh['row'=8,'col'=4] {'row','col'}, dimensions={0} | all-to-all | bytes 393216 | tf_op jit(solution)/shard_map/all_to_all | solution.py:163
  403.3 9.6 %reflect4.1 = (f32[1,1536]{1,0:T(1,128)}, f32[8,8,1536]{2,1,0:T(8,128)}, f32[8,8,1536]{2,1,0:T(8,128)}, f32[8,128]{1,0:T(8,128)}) custom-call(s32[1]{0:T(128)} %bitcast.col_ref, f32[8,8,1536]{2,1,0:T(8,128)} %bitcast.47, f32[4,8,1536]{2,1,0:T(8,128)} %bitcast.57, f32[8,8,1536]{2,1,0:T(8,128)} %get-tuple-element.62.upper_in, ...), custom_call_target="tpu_custom_call" | custom-call | tf_op jit(solution)/shard_map/reflect4/pallas_call | solution.py:137
  413.8 11.3 %all_to_all.52 = f32[32,1,1536]{2,1,0:T(1,128)S(1)} all-to-all(f32[32,1,1536]{2,1,0:T(1,128)S(1)} %broadcast_in_dim.58), channel_id=1, replica_groups=mesh['row'=8,'col'=4] {'row','col'}, dimensions={0} | all-to-all | bytes 393216 | tf_op jit(solution)/shard_map/all_to_all | solution.py:163
  426.4 9.6 %reflect5.1 = (f32[1,1536]{1,0:T(1,128)}, f32[8,8,1536]{2,1,0:T(8,128)}, f32[8,8,1536]{2,1,0:T(8,128)}, f32[8,128]{1,0:T(8,128)}) custom-call(s32[1]{0:T(128)} %bitcast.col_ref, f32[8,8,1536]{2,1,0:T(8,128)} %bitcast.48, f32[4,8,1536]{2,1,0:T(8,128)} %bitcast.58, f32[8,8,1536]{2,1,0:T(8,128)} %get-tuple-element.66.upper_in, ...), custom_call_target="tpu_custom_call" | custom-call | tf_op jit(solution)/shard_map/reflect5/pallas_call | solution.py:137
  436.8 11.3 %all_to_all.53 = f32[32,1,1536]{2,1,0:T(1,128)S(1)} all-to-all(f32[32,1,1536]{2,1,0:T(1,128)S(1)} %broadcast_in_dim.59), channel_id=1, replica_groups=mesh['row'=8,'col'=4] {'row','col'}, dimensions={0} | all-to-all | bytes 393216 | tf_op jit(solution)/shard_map/all_to_all | solution.py:163
  449.4 9.6 %reflect6.1 = (f32[1,1536]{1,0:T(1,128)}, f32[8,8,1536]{2,1,0:T(8,128)}, f32[8,8,1536]{2,1,0:T(8,128)}, f32[8,128]{1,0:T(8,128)}) custom-call(s32[1]{0:T(128)} %bitcast.col_ref, f32[8,8,1536]{2,1,0:T(8,128)} %bitcast.49, f32[4,8,1536]{2,1,0:T(8,128)} %bitcast.59, f32[8,8,1536]{2,1,0:T(8,128)} %get-tuple-element.70.upper_in, ...), custom_call_target="tpu_custom_call" | custom-call | tf_op jit(solution)/shard_map/reflect6/pallas_call | solution.py:137
  459.9 11.3 %all_to_all.54 = f32[32,1,1536]{2,1,0:T(1,128)S(1)} all-to-all(f32[32,1,1536]{2,1,0:T(1,128)S(1)} %broadcast_in_dim.60), channel_id=1, replica_groups=mesh['row'=8,'col'=4] {'row','col'}, dimensions={0} | all-to-all | bytes 393216 | tf_op jit(solution)/shard_map/all_to_all | solution.py:163
  472.5 9.7 %reflect7.1 = (f32[1,1536]{1,0:T(1,128)}, f32[8,8,1536]{2,1,0:T(8,128)}, f32[8,8,1536]{2,1,0:T(8,128)}, f32[8,128]{1,0:T(8,128)}) custom-call(s32[1]{0:T(128)} %bitcast.col_ref, f32[8,8,1536]{2,1,0:T(8,128)} %bitcast.50, f32[4,8,1536]{2,1,0:T(8,128)} %bitcast.60, f32[8,8,1536]{2,1,0:T(8,128)} %get-tuple-element.74.upper_in, ...), custom_call_target="tpu_custom_call" | custom-call | tf_op jit(solution)/shard_map/reflect7/pallas_call | solution.py:137
  483.6 2.6 all-to-all-start.7
  486.2 9.3 %all-to-all-done.7 = f32[32,1,1536]{2,1,0:T(1,128)S(1)} async-done(((f32[32,1,1536]{2,1,0:T(1,128)}), f32[32,1,1536]{2,1,0:T(1,128)S(1)}, u32[]{:S(2)}, u32[]{:S(2)}) %all-to-all-start.7) | async-done | bytes 196640 | tf_op jit(solution)/shard_map/all_to_all | solution.py:163
  496.8 3.5 reflect8.1
  (107 shorter events, 34.7 us)
Async XLA Ops:
  7.2 42.7 %all-gather.6.cloned.1.call-start = ((), (), s32[]{:S(2)}) async-start(), calls=%async_computation.8 | async-start | bytes 1966080 | tf_op jit(solution)/shard_map/all_gather | solution.py:189
  9.8 77.6 %all-gather.8.cloned.1.call-start = ((), (), s32[]{:S(2)}) async-start(), calls=%async_computation.9 | async-start | bytes 1966080 | tf_op jit(solution)/shard_map/all_gather | solution.py:189
  10.5 114.3 %all-gather.10.cloned.1.call-start = ((), (), s32[]{:S(2)}) async-start(), calls=%async_computation.10 | async-start | bytes 1966080 | tf_op jit(solution)/shard_map/all_gather | solution.py:189
  49.9 21.6 %collective-permute-start = (f32[1536,256]{1,0:T(8,128)}, f32[1536,256]{1,0:T(8,128)S(1)}, u32[]{:S(2)}, u32[]{:S(2)}) collective-permute-start(f32[1536,256]{1,0:T(8,128)} %all-gather.6.cloned.1.call-done), channel_id=1, source_target_pairs={{0,8},{4,20},{9,1},{13,29},{18,26},{22,6},{27,19},{31,15}} | collective-permute-start | bytes 4718600 | tf_op jit(solution)/shard_map/ppermute | solution.py:31
  71.5 99.0 %copy-start.4 = (f32[1536,256]{1,0:T(8,128)}, f32[1536,256]{1,0:T(8,128)S(1)}, u32[]{:S(2)}) copy-start(f32[1536,256]{1,0:T(8,128)S(1)} %collective-permute-done) | copy-start | bytes 4718596
  71.5 90.7 %all-gather.12.cloned.1.call-start = ((), (), s32[]{:S(2)}) async-start(), calls=%async_computation.11 | async-start | bytes 1966080 | tf_op jit(solution)/shard_map/all_gather | solution.py:189
  87.4 21.6 %collective-permute-start.2 = (f32[1536,256]{1,0:T(8,128)}, f32[1536,256]{1,0:T(8,128)S(1)}, u32[]{:S(2)}, u32[]{:S(2)}) collective-permute-start(f32[1536,256]{1,0:T(8,128)} %all-gather.8.cloned.1.call-done), channel_id=1, source_target_pairs={{0,8},{4,20},{9,1},{13,29},{18,26},{22,6},{27,19},{31,15}} | collective-permute-start | bytes 4718600 | tf_op jit(solution)/shard_map/ppermute | solution.py:31
  90.9 19.9 %collective-permute-start.1 = (f32[1536,256]{1,0:T(8,128)S(1)}, f32[1536,256]{1,0:T(8,128)}, u32[]{:S(2)}, u32[]{:S(2)}) collective-permute-start(f32[1536,256]{1,0:T(8,128)S(1)} %collective-permute-done), channel_id=1, source_target_pairs={{8,24},{20,28},{1,17},{29,21},{26,10},{6,14},{19,3},{15,7}} | collective-permute-start | bytes 4718600 | tf_op jit(solution)/shard_map/ppermute | solution.py:31
  109.0 61.5 %copy-start.5 = (f32[1536,256]{1,0:T(8,128)}, f32[1536,256]{1,0:T(8,128)S(1)}, u32[]{:S(2)}) copy-start(f32[1536,256]{1,0:T(8,128)S(1)} %collective-permute-done.2) | copy-start | bytes 4718596
  109.0 20.5 %collective-permute-start.5 = (f32[1536,256]{1,0:T(8,128)S(1)}, f32[1536,256]{1,0:T(8,128)}, u32[]{:S(2)}, u32[]{:S(2)}) collective-permute-start(f32[1536,256]{1,0:T(8,128)S(1)} %collective-permute-done.2), channel_id=1, source_target_pairs={{8,24},{20,28},{1,17},{29,21},{26,10},{6,14},{19,3},{15,7}} | collective-permute-start | bytes 4718600 | tf_op jit(solution)/shard_map/ppermute | solution.py:31
  124.9 41.9 %collective-permute-start.8 = (f32[1536,256]{1,0:T(8,128)}, f32[1536,256]{1,0:T(8,128)}, u32[]{:S(2)}, u32[]{:S(2)}) collective-permute-start(f32[1536,256]{1,0:T(8,128)} %all-gather.10.cloned.1.call-done), channel_id=1, source_target_pairs={{0,8},{4,20},{9,1},{13,29},{18,26},{22,6},{27,19},{31,15}} | collective-permute-start | bytes 4718600 | tf_op jit(solution)/shard_map/ppermute | solution.py:31
  129.5 41.1 %collective-permute-start.6 = (f32[1536,256]{1,0:T(8,128)}, f32[1536,256]{1,0:T(8,128)}, u32[]{:S(2)}, u32[]{:S(2)}) collective-permute-start(f32[1536,256]{1,0:T(8,128)} %collective-permute-done.5), channel_id=1, source_target_pairs={{24,16},{28,12},{17,25},{21,5},{10,2},{14,30},{3,11},{7,23}} | collective-permute-start | bytes 4718600 | tf_op jit(solution)/shard_map/ppermute | solution.py:31
  162.2 21.6 %collective-permute-start.12 = (f32[1536,256]{1,0:T(8,128)}, f32[1536,256]{1,0:T(8,128)}, u32[]{:S(2)}, u32[]{:S(2)}) collective-permute-start(f32[1536,256]{1,0:T(8,128)} %all-gather.12.cloned.1.call-done), channel_id=1, source_target_pairs={{0,8},{4,20},{9,1},{13,29},{18,26},{22,6},{27,19},{31,15}} | collective-permute-start | bytes 4718600 | tf_op jit(solution)/shard_map/ppermute | solution.py:31
  166.8 17.8 %collective-permute-start.9 = (f32[1536,256]{1,0:T(8,128)}, f32[1536,256]{1,0:T(8,128)}, u32[]{:S(2)}, u32[]{:S(2)}) collective-permute-start(f32[1536,256]{1,0:T(8,128)} %collective-permute-done.8), channel_id=1, source_target_pairs={{8,24},{20,28},{1,17},{29,21},{26,10},{6,14},{19,3},{15,7}} | collective-permute-start | bytes 4718600 | tf_op jit(solution)/shard_map/ppermute | solution.py:31
  168.6 16.8 %collective-permute-start.3 = (f32[1536,256]{1,0:T(8,128)}, f32[1536,256]{1,0:T(8,128)}, u32[]{:S(2)}, u32[]{:S(2)}) collective-permute-start(f32[1536,256]{1,0:T(8,128)} %collective-permute-done.1), channel_id=1, source_target_pairs={{24,16},{28,12},{17,25},{21,5},{10,2},{14,30},{3,11},{7,23}} | collective-permute-start | bytes 4718600 | tf_op jit(solution)/shard_map/ppermute | solution.py:31
  170.5 14.9 %copy-start.1 = (f32[1536,256]{1,0:T(8,128)S(1)}, f32[1536,256]{1,0:T(8,128)}, u32[]{:S(2)}) copy-start(f32[1536,256]{1,0:T(8,128)} %all-gather.6.cloned.1.call-done) | copy-start | bytes 4718596
  173.9 14.4 %collective-permute-start.7 = (f32[1536,256]{1,0:T(8,128)S(1)}, f32[1536,256]{1,0:T(8,128)}, u32[]{:S(2)}, u32[]{:S(2)}) collective-permute-start(f32[1536,256]{1,0:T(8,128)S(1)} %add_add_fusion.3), channel_id=1, source_target_pairs={{0,4},{4,0},{8,12},{12,8},{16,20},{20,16},{24,28},{28,24},{1,5},{5... | collective-permute-start | bytes 4718600 | tf_op jit(solution)/shard_map/ppermute | solution.py:46
  183.8 6.2 %collective-permute-start.13 = (f32[1536,256]{1,0:T(8,128)}, f32[1536,256]{1,0:T(8,128)S(1)}, u32[]{:S(2)}, u32[]{:S(2)}) collective-permute-start(f32[1536,256]{1,0:T(8,128)} %collective-permute-done.12), channel_id=1, source_target_pairs={{8,24},{20,28},{1,17},{29,21},{26,10},{6,14},{19,3},{15,7}} | collective-permute-start | bytes 4718600 | tf_op jit(solution)/shard_map/ppermute | solution.py:31
  184.6 17.4 %collective-permute-start.10 = (f32[1536,256]{1,0:T(8,128)}, f32[1536,256]{1,0:T(8,128)S(1)}, u32[]{:S(2)}, u32[]{:S(2)}) collective-permute-start(f32[1536,256]{1,0:T(8,128)} %collective-permute-done.9), channel_id=1, source_target_pairs={{24,16},{28,12},{17,25},{21,5},{10,2},{14,30},{3,11},{7,23}} | collective-permute-start | bytes 4718600 | tf_op jit(solution)/shard_map/ppermute | solution.py:31
  188.2 2.8 copy-start.3
  188.2 16.6 %collective-permute-start.4 = (f32[1536,256]{1,0:T(8,128)S(1)}, f32[1536,256]{1,0:T(8,128)S(1)}, u32[]{:S(2)}, u32[]{:S(2)}) collective-permute-start(f32[1536,256]{1,0:T(8,128)S(1)} %add_add_fusion.4), channel_id=1, source_target_pairs={{0,4},{4,0},{8,12},{12,8},{16,20},{20,16},{24,28},{28,24},{1,5},{5... | collective-permute-start | bytes 4718600 | tf_op jit(solution)/shard_map/ppermute | solution.py:46
  190.0 15.0 %collective-permute-start.14 = (f32[1536,256]{1,0:T(8,128)S(1)}, f32[1536,256]{1,0:T(8,128)S(1)}, u32[]{:S(2)}, u32[]{:S(2)}) collective-permute-start(f32[1536,256]{1,0:T(8,128)S(1)} %collective-permute-done.13), channel_id=1, source_target_pairs={{24,16},{28,12},{17,25},{21,5},{10,2},{14,30},{3,11},{7,23}} | collective-permute-start | bytes 4718600 | tf_op jit(solution)/shard_map/ppermute | solution.py:31
  191.0 11.0 %copy-start.2 = (f32[1536,256]{1,0:T(8,128)S(1)}, f32[1536,256]{1,0:T(8,128)}, u32[]{:S(2)}) copy-start(f32[1536,256]{1,0:T(8,128)} %all-gather.10.cloned.1.call-done) | copy-start | bytes 4718596
  204.3 1.4 copy-start
  204.3 14.6 %collective-permute-start.11 = (f32[1536,256]{1,0:T(8,128)S(1)}, f32[1536,256]{1,0:T(8,128)S(1)}, u32[]{:S(2)}, u32[]{:S(2)}) collective-permute-start(f32[1536,256]{1,0:T(8,128)S(1)} %add_add_fusion.2), channel_id=1, source_target_pairs={{0,4},{4,0},{8,12},{12,8},{16,20},{20,16},{24,28},{28,24},{1,5},{5... | collective-permute-start | bytes 4718600 | tf_op jit(solution)/shard_map/ppermute | solution.py:46
  207.5 22.7 %collective-permute-start.15 = (f32[1536,256]{1,0:T(8,128)S(1)}, f32[1536,256]{1,0:T(8,128)S(1)}, u32[]{:S(2)}, u32[]{:S(2)}) collective-permute-start(f32[1536,256]{1,0:T(8,128)S(1)} %add_add_fusion.1), channel_id=1, source_target_pairs={{0,4},{4,0},{8,12},{12,8},{16,20},{20,16},{24,28},{28,24},{1,5},{5... | collective-permute-start | bytes 4718600 | tf_op jit(solution)/shard_map/ppermute | solution.py:46
  230.2 1.4 copy-start.6
  266.7 28.5 %collective-permute-start.17 = (f32[8,1536]{1,0:T(8,128)S(1)}, f32[8,1536]{1,0:T(8,128)S(1)}, u32[]{:S(2)}, u32[]{:S(2)}) collective-permute-start(f32[8,1536]{1,0:T(8,128)S(1)} %copy.34), channel_id=1, source_target_pairs={{0,2},{4,6},{8,10},{12,14},{16,18},{20,22},{24,26},{28,30}} | collective-permute-start | bytes 147464 | tf_op jit(solution)/shard_map/ppermute | solution.py:206
  291.2 4.0 collective-permute-start.16
  292.5 3.0 collective-permute-start.18
  483.6 11.9 %all-to-all-start.7 = ((f32[32,1,1536]{2,1,0:T(1,128)}), f32[32,1,1536]{2,1,0:T(1,128)S(1)}, u32[]{:S(2)}, u32[]{:S(2)}) async-start(f32[32,1,1536]{2,1,0:T(1,128)} %broadcast_in_dim.61), calls=%async_computation.7 | async-start | bytes 393216 | tf_op jit(solution)/shard_map/all_to_all | solution.py:163
Sparse Core Ops, SparseCore 0:
  10.1 39.7 all-gather.5
  51.5 35.8 all-gather.7
  89.0 35.8 all-gather.9
  126.3 35.8 all-gather.11
